TPU v7x, 512 devices: a whole 4x4x16 slice. The times are simulated.
512 devices in a mesh: dp: 64 (over y, z_lo, core), inner: 8 (over z_hi, x).
Axes of the slice: x: 4, y: 4, z: 16 (z_hi: 2, z_lo: 8; z = z_hi * 8 + z_lo), core: 2. Of those that a mesh axis runs over, the one named last changes fastest.
Arguments:
- inputs: bfloat16 [512, 32, 32, 256], P(('dp', 'inner')), may hold values from -24 to 24
- cotangent: bfloat16 [512, 32, 32, 256], P(('dp', 'inner')), may hold values from -24 to 24
- kernel_taps: float32 [9, 256, 256], P(None, 'dp', 'inner'), may hold values from -1 to 1
Outputs:
- new_taps: float32 [9, 256, 256], P(None, 'dp', 'inner')
All inputs are finite; a program needn't handle non-finite values.
Results may differ from a plain program's by a relative error of at most 0.0003.
Values sent between devices are 32-bit elements; how exact they have to be, the bound alone decides.
A program may use at most 64 MiB of HBM per device.

v0:
```python
import functools
import math

import jax
import jax.numpy as jnp
from jax import lax
from jax.sharding import Mesh
from jax.sharding import PartitionSpec as P

MAPSIDE = 32
FREQS = 544
INNER = ("inner_0", "inner_1")
DP = ("dp_0", "dp_1", "dp_2")
DP_INNER = ("dp_0", "dp_1", "dp_2", "inner_0", "inner_1")


step_share = 0.06


def sum_in_order(pieces, axes, order):
    lengths = [lax.axis_size(a) for a in axes]
    pieces = pieces.reshape(*lengths, *pieces.shape[1:])
    pieces = pieces.transpose(*order, *range(len(axes), pieces.ndim))
    pieces = pieces.reshape(-1, *pieces.shape[len(axes) :])
    for k in order:
        pieces = lax.psum_scatter(pieces, axes[k], scatter_dimension=0, tiled=True)
    return pieces[0]


def in_blocks(value, dim, peers):
    before, after = (value.shape[:dim], value.shape[dim + 1 :])
    return jnp.moveaxis(value.reshape(*before, peers, -1, *after), dim, 0)


def sum_by_axis(value, axes, order, dim):
    peers = lax.axis_size(axes)
    return sum_in_order(in_blocks(value, dim, peers), axes, order)


def summed_on_arrival(value, axis, dim):
    pieces = in_blocks(value, dim, lax.axis_size(axis))
    arrived = lax.all_to_all(pieces, axis, split_axis=0, concat_axis=0, tiled=True)
    return arrived.sum(axis=0)


def over_axes(value, axes):
    return functools.reduce(lax.psum, axes, value)


def joined_along(pieces, dim):
    lengths = list(pieces.shape[1:])
    lengths[dim] *= pieces.shape[0]
    return jnp.moveaxis(pieces, 0, dim).reshape(lengths)


def from_everyone(value, axis):
    peers = lax.axis_size(axis)
    return lax.all_to_all(
        jnp.broadcast_to(value[None], (peers, *value.shape)), axis, 0, 0, tiled=True
    )


def gather_directly(value, axis, dim):
    return joined_along(from_everyone(value, axis), dim)


def one_exchange(value, axis, axes, splits, concats):
    sizes = [lax.axis_size(a) for a in axes]
    pieces = in_blocks(value, splits[0], sizes[0])
    pieces = jnp.moveaxis(in_blocks(pieces, splits[1] + 1, sizes[1]), 0, 1)
    inside = pieces.shape[2:]
    pieces = pieces.reshape(-1, *inside)
    pieces = lax.all_to_all(pieces, axis, split_axis=0, concat_axis=0, tiled=True)
    pieces = joined_along(pieces.reshape(*sizes, *inside), concats[0] + 1)
    return joined_along(pieces, concats[1])


def matmul(left_side, right_side):
    return jnp.dot(
        left_side, right_side, precision=lax.Precision.HIGHEST, preferred_element_type=jnp.float32
    )


def gradient_terms(inputs, cotangent):
    channels = inputs.shape[3]
    flat_cotangent = cotangent.reshape(-1, channels)
    collected = []
    for tap_index in range(9):
        row_off = tap_index // 3 - 1
        col_off = tap_index % 3 - 1
        shifted = jnp.roll(inputs, (-row_off, -col_off), axis=(1, 2))
        collected.append(
            lax.dot_general(
                shifted.reshape(-1, channels),
                flat_cotangent,
                (((0,), (0,)), ((), ())),
                preferred_element_type=jnp.float32,
            )
        )
    return jnp.stack(collected)


def phase_tables(freq_index, mapside, freq_count):
    row_shift = jnp.array([-1, -1, -1, 0, 0, 0, 1, 1, 1], dtype=jnp.int32)
    col_shift = jnp.array([-1, 0, 1, -1, 0, 1, -1, 0, 1], dtype=jnp.int32)
    half_width = mapside // 2 + 1
    first_freq = freq_index // half_width
    second_freq = freq_index % half_width
    turn_count = (
        first_freq[:, None] * row_shift[None, :] + second_freq[:, None] * col_shift[None, :]
    ) % mapside
    phase_angle = turn_count.astype(jnp.float32) * (2.0 * math.pi / mapside)
    live_mask = (freq_index < freq_count).astype(jnp.float32)[:, None]
    return (jnp.cos(phase_angle) * live_mask, jnp.sin(phase_angle) * live_mask)


def inverse_tables(freq_index, mapside, freq_count):
    cos_table, sin_table = phase_tables(freq_index, mapside, freq_count)
    second_freq = freq_index % (mapside // 2 + 1)
    on_edge = (second_freq == 0) | (second_freq == mapside // 2)
    weight = jnp.where(on_edge, 1.0, 2.0).astype(jnp.float32) / (mapside * mapside)
    return (cos_table * weight[:, None], sin_table * weight[:, None])


def bjorck(real_part, imag_part):
    matrix_size = real_part.shape[0]
    identity = jnp.eye(matrix_size, dtype=jnp.float32)
    for iteration in range(2):
        products = matmul(real_part.T, jnp.concatenate([real_part, imag_part], axis=1))
        square = matmul(imag_part.T, imag_part)
        cross_part = products[:, matrix_size:]
        gram_real = products[:, :matrix_size] + square
        gram_imag = cross_part - cross_part.T
        mix_real = 1.5 * identity - 0.5 * gram_real
        mix_imag = -0.5 * gram_imag
        stacked = jnp.concatenate(
            [
                jnp.concatenate([mix_real, mix_imag], axis=1),
                jnp.concatenate([-mix_imag, mix_real], axis=1),
            ],
            axis=0,
        )
        joined = matmul(jnp.concatenate([real_part, imag_part], axis=1), stacked)
        real_part, imag_part = (joined[:, :matrix_size], joined[:, matrix_size:])
    return (real_part, imag_part)


def orthonormalize(matrices):
    return bjorck(matrices[0], matrices[1])


def body(inputs, cotangent, kernel_taps):
    channels = inputs.shape[3]
    local_terms = gradient_terms(inputs, cotangent)
    partial_sum = sum_by_axis(local_terms, INNER, (1, 0), 2)
    gradient = summed_on_arrival(partial_sum, DP, 1)
    square_sum = over_axes(jnp.sum(gradient * gradient), DP_INNER)
    step_factor = step_share * math.sqrt(channels) / (jnp.sqrt(square_sum) + 1e-06)
    updated = kernel_taps - step_factor * gradient
    wide_count = lax.axis_size(DP)
    narrow = lax.axis_size(INNER)
    freq_dev = -(-FREQS // (wide_count * narrow))
    in_rows = updated.shape[1]
    out_cols = updated.shape[2]
    col_blocks = gather_directly(updated, INNER, 2)
    gathered = lax.all_gather(col_blocks, DP, axis=1, tiled=True)
    linear = lax.axis_index(DP) * narrow + lax.axis_index(INNER)
    owned_freq = linear * freq_dev + jnp.arange(freq_dev, dtype=jnp.int32)
    cos_table, sin_table = phase_tables(owned_freq, MAPSIDE, FREQS)
    flattened = gathered.reshape(9, channels * channels)
    real_part = matmul(cos_table, flattened).reshape(freq_dev, channels, channels)
    imag_part = -matmul(sin_table, flattened).reshape(freq_dev, channels, channels)
    real_part, imag_part = lax.map(orthonormalize, (real_part, imag_part))
    returned = one_exchange(
        jnp.stack([real_part, imag_part], axis=1), DP_INNER, (DP, INNER), (2, 3), (0, 0)
    )
    slot_count = returned.shape[0]
    slot_index = jnp.arange(slot_count, dtype=jnp.int32)
    from_narrow = slot_index // (wide_count * freq_dev)
    from_wide = slot_index // freq_dev % wide_count
    freq_index = (from_wide * narrow + from_narrow) * freq_dev + slot_index % freq_dev
    weighted_cos, weighted_sin = inverse_tables(freq_index, MAPSIDE, FREQS)
    rebuilt = matmul(weighted_cos.T, returned[:, 0].reshape(slot_count, -1)) - matmul(
        weighted_sin.T, returned[:, 1].reshape(slot_count, -1)
    )
    return (math.sqrt(channels) * rebuilt).reshape(9, in_rows, out_cols)


def solution(mesh):
    torus = Mesh(
        mesh.devices.reshape(4, 8, 2, 2, 4), ("dp_0", "dp_1", "dp_2", "inner_0", "inner_1")
    )
    return jax.shard_map(
        body,
        mesh=torus,
        in_specs=(P(DP_INNER, None, None, None), P(DP_INNER, None, None, None), P(None, DP, INNER)),
        out_specs=P(None, DP, INNER),
        check_vma=False,
    )
```

profile of v0, /device:TPU:1, one launch (start us, length us, event | category | flops | bytes accessed | tf_op | source)
XLA Modules:
  0.0 517.9 jit_solution(3652921632842971304)
XLA Ops:
  29.2 44.8 %reduce-scatter.3.cloned.1.call-done = f32[2,9,256,32]{2,3,1,0:T(8,128)} async-done(((f32[8,9,256,32]{2,3,1,0:T(8,128)}), f32[2,9,256,32]{2,3,1,0:T(8,128)}) %reduce-scatter.3.cloned.1.call-update) | async-done | bytes 589840 | tf_op jit(solution)/shard_map/reduce_scatter | solution.py:26
  74.1 56.5 %reduce-scatter.5.cloned.1.call-done = f32[1,9,256,32]{2,3,1,0:T(8,128)} async-done(((f32[2,9,256,32]{2,3,1,0:T(8,128)}), f32[1,9,256,32]{2,3,1,0:T(8,128)}) %reduce-scatter.5.cloned.1.call-update) | async-done | bytes 294928 | tf_op jit(solution)/shard_map/reduce_scatter | solution.py:26
  132.9 26.3 %all_to_all.15 = f32[64,1,1152]{2,1,0:T(1,128)S(1)} all-to-all(f32[64,1,1152]{2,1,0:T(1,128)S(1)} %reshape.279), channel_id=1, replica_groups=mesh['dp_0'=4,'dp_1'=8,'dp_2'=2,'inner_0'=2,'inner_1'=4] {'dp_0','dp_1',..., dimensions={0} | all-to-all | bytes 589824 | tf_op jit(solution)/shard_map/all_to_all | solution.py:42
  162.6 7.7 %psum.35 = f32[]{:T(128)} all-reduce(f32[]{:T(128)} %multiply_reduce_fusion), channel_id=1, replica_groups=mesh['dp_0'=4,'dp_1'=8,'dp_2'=2,'inner_0'=2,'inner_1'=4] {'dp_0'}, use_global_device_ids=true, to_apply=%region_4.5 | all-reduce | flops 1 | bytes 8 | tf_op jit(solution)/shard_map/psum | solution.py:47
  170.3 24.8 %psum.36 = f32[]{:T(128)} all-reduce(f32[]{:T(128)} %psum.35), channel_id=1, replica_groups=mesh['dp_0'=4,'dp_1'=8,'dp_2'=2,'inner_0'=2,'inner_1'=4] {'dp_1'}, use_global_device_ids=true, to_apply=%region_5.6 | all-reduce | flops 1 | bytes 8 | tf_op jit(solution)/shard_map/psum | solution.py:47
  195.1 8.8 %psum.37 = f32[]{:T(128)} all-reduce(f32[]{:T(128)} %psum.36), channel_id=1, replica_groups=mesh['dp_0'=4,'dp_1'=8,'dp_2'=2,'inner_0'=2,'inner_1'=4] {'dp_2'}, use_global_device_ids=true, to_apply=%region_6.7 | all-reduce | flops 1 | bytes 8 | tf_op jit(solution)/shard_map/psum | solution.py:47
  203.9 13.1 %psum.38 = f32[]{:T(128)} all-reduce(f32[]{:T(128)} %psum.37), channel_id=1, replica_groups=mesh['dp_0'=4,'dp_1'=8,'dp_2'=2,'inner_0'=2,'inner_1'=4] {'inner_0'}, use_global_device_ids=true, to_apply=%region_7.8 | all-reduce | flops 1 | bytes 8 | tf_op jit(solution)/shard_map/psum | solution.py:47
  217.0 9.0 %psum.39 = f32[]{:T(128)} all-reduce(f32[]{:T(128)} %psum.38), channel_id=1, replica_groups=mesh['dp_0'=4,'dp_1'=8,'dp_2'=2,'inner_0'=2,'inner_1'=4] {'inner_1'}, use_global_device_ids=true, to_apply=%region_8.9 | all-reduce | flops 1 | bytes 8 | tf_op jit(solution)/shard_map/psum | solution.py:47
  227.0 21.6 %all_to_all.16 = f32[8,1,1152]{2,1,0:T(1,128)S(1)} all-to-all(f32[8,1,1152]{2,1,0:T(1,128)S(1)} %reshape.281), channel_id=1, replica_groups=mesh['dp_0'=4,'dp_1'=8,'dp_2'=2,'inner_0'=2,'inner_1'=4] {'inner_0','inn..., dimensions={0} | all-to-all | bytes 73728 | tf_op jit(solution)/shard_map/all_to_all | solution.py:58
  250.3 114.2 %all-gather.2.cloned.1.call-done = f32[9,256,256]{2,0,1:T(8,128)} async-done(((f32[9,4,256]{2,0,1:T(8,128)}), f32[9,256,256]{2,0,1:T(8,128)}) %all-gather.2.cloned.1.call-update) | async-done | bytes 2359312 | tf_op jit(solution)/shard_map/all_gather | solution.py:166
  364.5 3.6 copy.156
  368.7 3.5 fusion.33
  372.2 3.5 fusion.31
  375.7 26.9 %while.12 = (s32[]{:T(128)}, f32[2,256,256]{2,0,1:T(2,128)S(1)}, f32[2,256,256]{2,0,1:T(2,128)}, f32[2,256,256]{2,0,1:T(2,128)S(1)}, f32[2,256,256]{2,0,1:T(2,128)S(1)}, /*index=5*/s32[]{:T(128)}, s32[]{:T(128)}) while((s32[]{:T(128)}, f32[2,256,256]{2,0,1:T(2,128)S(1)}, f32[2,256,256]{2,0,1:T(2,128)}, f32[2,256,256]{2,0,1:T(2,128)S(1)}, ...), condition=%wide.region_10.11_spmd, body=%wide.region_9.10_spmd.sunk | while | flops 2821455872 | bytes 21233808 | solution.py:173
  381.9 3.5 dynamic_update_slice.10
  385.7 3.5 dynamic_update_slice.9
  395.3 3.5 dynamic_update_slice.10
  399.1 3.5 dynamic_update_slice.9
  408.7 6.8 %copy.165 = f32[512,2,2,4,32]{4,3,2,1,0:T(4,128)} copy(f32[512,2,2,4,32]{4,0,3,2,1:T(8,128)} %bitcast.232) | data formatting | bytes 2097152 | tf_op jit(solution)/shard_map/reshape | solution.py:72
  415.5 5.3 %reshape.283 = f32[512,1,512]{2,1,0:T(1,128)} reshape(f32[512,2,2,4,32]{4,3,2,1,0:T(4,128)} %copy.165) | data formatting | bytes 2097152
  420.8 14.1 %all-to-all-start.2 = ((f32[512,1,512]{2,1,0:T(1,128)}), f32[512,1,512]{2,1,0:T(1,128)S(1)}, u32[]{:S(2)}, u32[]{:S(2)}) async-start(f32[512,1,512]{2,1,0:T(1,128)} %reshape.283), calls=%async_computation.4 | async-start | bytes 2097152 | tf_op jit(solution)/shard_map/all_to_all | solution.py:73
  435.0 58.3 %all-to-all-done.2 = f32[512,1,512]{2,1,0:T(1,128)S(1)} async-done(((f32[512,1,512]{2,1,0:T(1,128)}), f32[512,1,512]{2,1,0:T(1,128)S(1)}, u32[]{:S(2)}, u32[]{:S(2)}) %all-to-all-start.2) | async-done | bytes 1048608 | tf_op jit(solution)/shard_map/all_to_all | solution.py:73
  496.5 3.5 reshape.284
  500.0 4.3 copy.166
  (127 shorter events, 58.8 us)
Async XLA Ops:
  6.5 67.5 %reduce-scatter.3.cloned.1.call-start = ((), (), s32[]{:S(2)}) async-start(), calls=%async_computation.5 | async-start | bytes 2949120 | tf_op jit(solution)/shard_map/reduce_scatter | solution.py:26
  7.8 3.8 copy-start.1
  7.9 2.5 copy-start
  17.7 2.7 copy-start.2
  17.7 2.7 copy-start.3
  20.4 1.0 copy-start.10
  21.1 1.1 copy-start.11
  23.1 1.0 copy-start.9
  23.8 1.1 copy-start.8
  25.7 1.0 copy-start.7
  29.1 101.4 %reduce-scatter.5.cloned.1.call-start = ((), (), s32[]{:S(2)}) async-start(), calls=%async_computation.6 | async-start | bytes 884736 | tf_op jit(solution)/shard_map/reduce_scatter | solution.py:26
  74.0 290.4 %all-gather.2.cloned.1.call-start = ((), (), s32[]{:S(2)}) async-start(), calls=%async_computation.7 | async-start | bytes 4259840 | tf_op jit(solution)/shard_map/all_gather | solution.py:166
  132.1 94.7 %copy-start.12 = (f32[9,4,32]{2,1,0:T(4,128)S(1)}, f32[9,4,32]{2,1,0:T(4,128)}, u32[]{:S(2)}) copy-start(f32[9,4,32]{2,1,0:T(4,128)} %param.11) | copy-start | bytes 13828
  368.1 0.7 copy-start.13
  368.1 0.7 copy-start.14
  379.9 2.0 copy-start.5
  385.4 3.8 copy-start.6
  393.2 2.0 copy-start.5
  398.8 3.8 copy-start.6
  402.6 0.8 copy-start.4
  420.8 72.5 %all-to-all-start.2 = ((f32[512,1,512]{2,1,0:T(1,128)}), f32[512,1,512]{2,1,0:T(1,128)S(1)}, u32[]{:S(2)}, u32[]{:S(2)}) async-start(f32[512,1,512]{2,1,0:T(1,128)} %reshape.283), calls=%async_computation.4 | async-start | bytes 2097152 | tf_op jit(solution)/shard_map/all_to_all | solution.py:73
Sparse Core Ops, SparseCore 0:
  29.3 44.7 reduce-scatter.2
  76.8 53.6 reduce-scatter.4
  250.3 114.1 all-gather.1
where the time goes:
time: 527 us; the launch traced here: 518 us
  waiting for transfers between devices  274 us (52%)
  blocking collectives  111 us (21%)
  local copies, waits for them, and re-layouts  67.2 us (13%)
  matrix products  26.4 us (5%)
  between operations  14.6 us (3%)
  starting transfers between devices  14.2 us (3%)
  other arithmetic  9.74 us (2%)
    all_gather x1, waiting for transfers between devices, body(): gathered = lax.all_gather(col_blocks, DP, axis=1, tiled=True)  114 us
    reduce_scatter x2, waiting for transfers between devices, sum_in_order(): pieces = lax.psum_scatter(pieces, axes[k], scatter_dimension=0, tiled=True)  101 us
    psum x5, blocking collectives, over_axes(): return functools.reduce(lax.psum, axes, value)  63.5 us
    all_to_all x1, waiting for transfers between devices, one_exchange(): lax.all_to_all(pieces, axis, split_axis=0, concat_axis=0, tiled=True)  58.3 us
    all_to_all x1, blocking collectives, summed_on_arrival(): lax.all_to_all(pieces, axis, split_axis=0, concat_axis=0, tiled=True)  26.3 us
    all_to_all x1, blocking collectives, from_everyone(): lax.all_to_all(jnp.broadcast_to(value[None], (peers, *value.shape)), axis...  21.6 us
    dot_general x16, matrix products, matmul(): jnp.dot(left_side, right_side, precision=lax.Precision.HIGHEST, preferred...  17.6 us
    dynamic_update_slice x8, local copies, waits for them, and re-layouts, body(): real_part, imag_part = lax.map(orthonormalize, (real_part, imag_part))  15.2 us
  transfers between devices with their start and end apart: 4, of which 4 were waited for; matrix products, arithmetic and copies ran while one was open for 0% of the time, Pallas kernels for 0%

commit v1 on v0

v1 whole, which is shorter than its diff:
```python
import functools
import math

import jax
import jax.numpy as jnp
from jax import lax
from jax.experimental import pallas as pl
from jax.experimental.pallas import tpu as pltpu
from jax.sharding import Mesh
from jax.sharding import PartitionSpec as P

AXES = ("dp_0", "dp_1", "dp_2", "inner_0", "inner_1")
INNER = ("inner_0", "inner_1")
DP = ("dp_0", "dp_1", "dp_2")
DP_INNER = DP + INNER
SIDE = 32
CHANNELS = 256
CELLS = SIDE * SIDE
STEP = 0.06 * math.sqrt(CHANNELS)
F32 = jnp.float32
BF16 = jnp.bfloat16
PLANE = 32
DEPTH = 16
CHUNKS = 3
MESH = pl.DeviceIdType.MESH
COS = [math.cos(2.0 * math.pi * k / SIDE) for k in range(SIDE)]
SIN = [math.sin(2.0 * math.pi * k / SIDE) for k in range(SIDE)]


def swap_groups(parts):
    lane = lax.broadcasted_iota(jnp.int32, parts[0].shape, 1)
    low = lane < 64
    even = (lane & 32) == 0
    v0, v1, v2, v3 = parts
    w0 = jnp.where(low, v0, pltpu.roll(v2, 64, 1))
    w2 = jnp.where(low, pltpu.roll(v0, 64, 1), v2)
    w1 = jnp.where(low, v1, pltpu.roll(v3, 64, 1))
    w3 = jnp.where(low, pltpu.roll(v1, 64, 1), v3)
    u0 = jnp.where(even, w0, pltpu.roll(w1, 32, 1))
    u1 = jnp.where(even, pltpu.roll(w0, 96, 1), w1)
    u2 = jnp.where(even, w2, pltpu.roll(w3, 32, 1))
    u3 = jnp.where(even, pltpu.roll(w2, 96, 1), w3)
    return u0, u1, u2, u3


def halves(value):
    high = value.astype(BF16)
    low = (value - high.astype(F32)).astype(BF16)
    return high, low


def product(left, right):
    dot = functools.partial(jnp.dot, preferred_element_type=F32)
    return dot(left[0], right[0]) + (dot(left[0], right[1]) + dot(left[1], right[0]))


def kernel(x_ref, ct_ref, taps_ref, out_ref, xt, cb, go, gr, s0, s1, r0, r1, t0, t1, u0, u1, zs, zr, gs, as_t, ar_t,
           as_g, ar_g, nv, nr, ks_t, kr_t, ks_g, kr_g, mat, ao, ar, fs, fr, pair_send, pair_recv, a_send, a_recv,
           b_send, b_recv, c_send, c_recv, one_send, one_recv):
    y = lax.axis_index("dp_0")
    zl = lax.axis_index("dp_1")
    c = lax.axis_index("dp_2")
    zh = lax.axis_index("inner_0")
    x = lax.axis_index("inner_1")
    z = zh * 8 + zl
    p = (y * 2 + c) * 4 + x

    def at_plane(q):
        return (q // 8, zl, (q // 4) % 2, zh, q % 4)

    def at_depth(w):
        return (y, w % 8, c, w // 8, x)

    def send(src, dst, send_sem, recv_sem, device):
        pltpu.make_async_remote_copy(
            src_ref=src, dst_ref=dst, send_sem=send_sem, recv_sem=recv_sem, device_id=device, device_id_type=MESH
        ).start()

    def drain(ref, sem):
        pltpu.make_async_copy(ref, ref, sem).wait()

    barrier = pltpu.get_barrier_semaphore()
    for d in range(1, PLANE):
        pl.semaphore_signal(barrier, inc=1, device_id=at_plane((p + d) % PLANE), device_id_type=MESH)
    for d in range(1, DEPTH):
        pl.semaphore_signal(barrier, inc=1, device_id=at_depth((z + d) % DEPTH), device_id_type=MESH)

    row = lax.broadcasted_iota(jnp.int32, (256, 256), 0)
    col = lax.broadcasted_iota(jnp.int32, (256, 256), 1)
    channel = (row & 192) + (row & 7) * 8 + ((row >> 5) & 1) * 4 + ((row >> 3) & 3)
    order = jnp.where(col == channel, 1.0, 0.0).astype(BF16)
    for k in range(4):
        xt[:, k * 256 : (k + 1) * 256] = lax.dot_general(
            order, x_ref[k * 256 : (k + 1) * 256, :], (((1,), (1,)), ((), ())), preferred_element_type=F32
        ).astype(BF16)
    for m in range(3):
        source = (row & 224) + ((row + (33 - m)) & 31)
        shift = jnp.where(col == source, 1.0, 0.0).astype(BF16)
        for k in range(4):
            rows = ct_ref[k * 256 : (k + 1) * 256, :]
            if m != 1:
                rows = jnp.dot(shift, rows, preferred_element_type=F32).astype(BF16)
            cb[m, 32 + k * 256 : 32 + (k + 1) * 256, :] = rows
        cb[m, 0:32, :] = cb[m, 1024:1056, :]
        cb[m, 1056:1088, :] = cb[m, 32:64, :]

    def depth_messages(block, dst):
        before, middle, after = [
            jnp.concatenate([block[3 * a + b : 3 * a + b + 1, :] for a in range(3)], axis=0) for b in range(3)
        ]
        both = after + before
        apart = after - before
        for w in range(DEPTH):
            if w == 0:
                upper, lower = middle + both, middle - both
            else:
                upper, lower = middle + COS[w] * both, -SIN[w] * apart
            dst[8 * w : 8 * w + 3, :] = upper
            dst[8 * w + 3 : 8 * w + 6, :] = lower
        return None

    def depth_send(src, dst, sem):
        for d in range(1, DEPTH):
            w = (z + d) % DEPTH
            send(src.at[pl.ds(pl.multiple_of(w * 8, 8), 8)], dst.at[pl.ds(pl.multiple_of(z * 8, 8), 8)],
                 one_send.at[sem], one_recv.at[sem], at_depth(w))
        own = pl.ds(pl.multiple_of(z * 8, 8), 8)
        dst[own, :] = src[own, :]

    def depth_wait(dst, sem):
        drain(dst.at[pl.ds(0, 120)], one_recv.at[sem])

    def plane_messages(src, dst):
        parts = [src[pl.ds(m, DEPTH, stride=8), :] for m in range(6)]

        @pl.when(z != 0)
        def _():
            real_sum, real_gap = parts[2] + parts[0], parts[2] - parts[0]
            imag_sum, imag_gap = parts[5] + parts[3], parts[5] - parts[3]
            for k in range(17):
                upper, upper_gap = parts[1] + COS[k] * real_sum, SIN[k] * imag_gap
                lower, lower_gap = parts[4] + COS[k] * imag_sum, SIN[k] * real_gap
                dst[k, 0:16, :] = upper + upper_gap
                dst[k, 16:32, :] = lower - lower_gap
                if 0 < k < 16:
                    dst[32 - k, 0:16, :] = upper - upper_gap
                    dst[32 - k, 16:32, :] = lower + lower_gap

        @pl.when(z == 0)
        def _():
            for half in range(2):
                first, mid, last = parts[3 * half : 3 * half + 3]
                total, gap = last + first, last - first
                dst[16 * half, 0:16, :] = mid + total
                dst[16 * half, 16:32, :] = mid - total
                for k in range(1, 16):
                    dst[16 * half + k, 0:16, :] = mid + COS[k] * total
                    dst[16 * half + k, 16:32, :] = -SIN[k] * gap

    def plane_send(src, dst, sem):
        for d in range(1, PLANE):
            q = (p + d) % PLANE
            send(src.at[q], dst.at[p], one_send.at[sem], one_recv.at[sem], at_plane(q))
        dst[p] = src[p]

    def plane_wait(dst, sem):
        drain(dst.at[pl.ds(0, PLANE - 1)], one_recv.at[sem])

    as_t[...] = jnp.zeros_like(as_t)
    as_g[...] = jnp.zeros_like(as_g)
    fs[...] = jnp.zeros_like(fs)
    depth_messages(taps_ref[...], as_t)

    def chunk_out(ch):
        for t in range(3):
            drain(gr.at[3 * ch + t], pair_recv.at[3 * ch + t])
        for t in range(3):
            for yy in range(4):
                for xx in range(4):
                    s0[ch, xx, t, yy] = go[c, 3 * ch + t, yy, xx, 0] + gr[3 * ch + t, yy, xx, 0]
                    s1[ch, yy, t, xx] = go[c, 3 * ch + t, yy, xx, 1] + gr[3 * ch + t, yy, xx, 1]
        for d in (1, 3, 2):
            xx, yy = (x + d) % 4, (y + d) % 4
            send(s0.at[ch, xx], r0.at[ch, d - 1], a_send.at[0], a_recv.at[ch], (y, zl, c, zh, xx))
            send(s1.at[ch, yy], r1.at[ch, d - 1], a_send.at[1], a_recv.at[3 + ch], (yy, zl, c, zh, x))

    def chunk_on(ch):
        drain(r0.at[ch], a_recv.at[ch])
        for t in range(3):
            for yy in range(4):
                t0[ch, yy, t] = (s0[ch, x, t, yy] + r0[ch, 0, t, yy]) + (r0[ch, 1, t, yy] + r0[ch, 2, t, yy])
        for d in (1, 3, 2):
            yy = (y + d) % 4
            send(t0.at[ch, yy], u0.at[ch, d - 1], b_send.at[0], b_recv.at[ch], (yy, zl, c, zh, x))
        drain(r1.at[ch], a_recv.at[3 + ch])
        for t in range(3):
            for xx in range(4):
                t1[ch, xx, t] = (s1[ch, y, t, xx] + r1[ch, 0, t, xx]) + (r1[ch, 1, t, xx] + r1[ch, 2, t, xx])
        for d in (1, 3, 2):
            xx = (x + d) % 4
            send(t1.at[ch, xx], u1.at[ch, d - 1], b_send.at[1], b_recv.at[3 + ch], (y, zl, c, zh, xx))

    def chunk_in(ch):
        drain(u0.at[ch], b_recv.at[ch])
        drain(u1.at[ch], b_recv.at[3 + ch])
        for t in range(3):
            first = (t0[ch, y, t] + u0[ch, 0, t]) + (u0[ch, 1, t] + u0[ch, 2, t])
            second = (t1[ch, x, t] + u1[ch, 0, t]) + (u1[ch, 1, t] + u1[ch, 2, t])
            for w in range(8):
                zs[w, 3 * ch + t : 3 * ch + t + 1, :] = first[w : w + 1, :]
                zs[8 + w, 3 * ch + t : 3 * ch + t + 1, :] = second[w : w + 1, :]

    for t in range(9):
        a, b = t // 3 - 1, t % 3
        grad = jnp.dot(xt[...], cb[b, 32 - 32 * a : 32 - 32 * a + CELLS, :], preferred_element_type=F32)
        for yc in range(8):
            for h in range(2):
                parts = [grad[yc * 32 + i * 8 : yc * 32 + i * 8 + 8, h * 128 : h * 128 + 128] for i in range(4)]
                for xx, part in enumerate(swap_groups(parts)):
                    go[yc % 2, t, yc // 2, xx, h] = part
        if t == 0:
            pl.semaphore_wait(barrier, PLANE + DEPTH - 2)
            depth_send(as_t, ar_t, 0)
        send(go.at[1 - c, t], gr.at[t], pair_send, pair_recv.at[t], (y, zl, 1 - c, zh, x))
        if t == 4:
            chunk_out(0)
        if t == 7:
            chunk_out(1)
    chunk_out(2)
    for ch in range(CHUNKS):
        chunk_on(ch)
    depth_wait(ar_t, 0)
    plane_messages(ar_t, ks_t)
    plane_send(ks_t, kr_t, 2)
    for ch in range(CHUNKS):
        chunk_in(ch)

    for d in range(1, DEPTH):
        w = (z + d) % DEPTH
        send(zs.at[w], zr.at[d - 1], c_send, c_recv, at_depth(w))
    drain(zr, c_recv)
    block = zs[z]
    for d in range(DEPTH - 1):
        block = block + zr[d]
    gs[...] = block
    depth_messages(gs[...], as_g)
    squares = jnp.sum(block * block, axis=0, keepdims=True)
    for w in range(DEPTH):
        as_g[8 * w + 6 : 8 * w + 7, :] = squares
    depth_send(as_g, ar_g, 1)
    depth_wait(ar_g, 1)

    nv[...] = jnp.sum(ar_g[pl.ds(6, DEPTH, stride=8), :], axis=0, keepdims=True)
    for d in range(1, PLANE):
        q = (p + d) % PLANE
        send(nv, nr.at[d - 1], one_send.at[6], one_recv.at[6], at_plane(q))
    plane_messages(ar_g, ks_g)
    plane_send(ks_g, kr_g, 3)
    plane_wait(kr_t, 2)
    drain(nr, one_recv.at[6])
    total = nv[...]
    for d in range(PLANE - 1):
        total = total + nr[d]
    norm = jnp.sqrt(jnp.sum(total, axis=1, keepdims=True))
    factor = jnp.broadcast_to(STEP / (norm + 1e-6), (8, 128))
    plane_wait(kr_g, 3)

    for yc in range(8):
        for m in range(2):
            for h in range(2):
                rows = slice(m * 16 + h * 8, m * 16 + h * 8 + 8)
                parts = [kr_t[yc * 4 + xx, rows, :] - factor * kr_g[yc * 4 + xx, rows, :] for xx in range(4)]
                for i, part in enumerate(swap_groups(parts)):
                    mat[m, yc * 32 + i * 8 : yc * 32 + i * 8 + 8, h * 128 : h * 128 + 128] = part

    joint = jnp.where((z == 0) & (p % 16 == 0), 0.0, 1.0).astype(F32)
    for _ in range(2):
        real, imag = mat[0], mat[1]
        real_2, imag_2 = halves(real), halves(imag)
        real_t, imag_t = halves(real.T), halves(imag.T)
        first = product(real_t, real_2)
        second = product(imag_t, imag_2)
        cross = product(real_t, imag_2) - product(imag_t, real_2)
        eye = jnp.where(row == col, 1.5, 0.0)
        mix_first = halves(eye - 0.5 * (first + joint * second))
        mix_second = halves(eye - 0.5 * (second + joint * first))
        mix_cross = halves((-0.5 * joint) * cross)
        mat[0] = product(real_2, mix_first) - product(imag_2, mix_cross)
        mat[1] = product(real_2, mix_cross) + product(imag_2, mix_second)

    for yc in range(8):
        for m in range(2):
            for h in range(2):
                parts = [mat[m, yc * 32 + i * 8 : yc * 32 + i * 8 + 8, h * 128 : h * 128 + 128] for i in range(4)]
                for xx, part in enumerate(swap_groups(parts)):
                    ao[yc * 4 + xx, m * 16 + h * 8 : m * 16 + h * 8 + 8, :] = part
    plane_send(ao, ar, 4)
    plane_wait(ar, 4)

    def summed(first, last, base):
        zero = jnp.zeros((DEPTH, 128), F32)
        real_0 = imag_0 = real_c = real_s = imag_c = imag_s = zero
        for k in range(first, last):
            real, imag = ar[k, 0:16, :], ar[k, 16:32, :]
            ck, sk = COS[k - base], SIN[k - base]
            real_0, imag_0 = real_0 + real, imag_0 + imag
            real_c, real_s = real_c + ck * real, real_s + sk * real
            imag_c, imag_s = imag_c + ck * imag, imag_s + sk * imag
        return real_0, imag_0, real_c, real_s, imag_c, imag_s

    @pl.when(z != 0)
    def _():
        real_0, imag_0, real_c, real_s, imag_c, imag_s = summed(0, 32, 0)
        parts = (real_c + imag_s, real_0, real_c - imag_s, imag_c - real_s, imag_0, imag_c + real_s)
        for m, part in enumerate(parts):
            fs[pl.ds(m, DEPTH, stride=8), :] = 2.0 * part

    @pl.when(z == 0)
    def _():
        for half in range(2):
            real_0, imag_0, real_c, real_s, imag_c, imag_s = summed(16 * half + 1, 16 * half + 16, 16 * half)
            one, other = ar[16 * half, 0:16, :], ar[16 * half, 16:32, :]
            parts = (
                2.0 * (real_c + imag_s) + (one - other),
                2.0 * real_0 + (one + other),
                2.0 * (real_c - imag_s) + (one - other),
            )
            for m, part in enumerate(parts):
                fs[pl.ds(3 * half + m, DEPTH, stride=8), :] = part

    depth_send(fs, fr, 5)
    depth_wait(fr, 5)
    plain = fr[8:16, :]
    cosine = COS[1] * fr[8:16, :]
    sine = SIN[1] * fr[8:16, :]
    for w in range(2, DEPTH):
        tile = fr[8 * w : 8 * w + 8, :]
        plain, cosine, sine = plain + tile, cosine + COS[w] * tile, sine + SIN[w] * tile
    edge = fr[0:8, :]
    for a in range(3):
        first, last = edge[a : a + 1, :], edge[a + 3 : a + 4, :]
        even, odd = first + last, first - last
        out_ref[3 * a + 1 : 3 * a + 2, :] = (plain[a : a + 1, :] + even) * (1.0 / 64.0)
        out_ref[3 * a : 3 * a + 1, :] = (cosine[a : a + 1, :] + sine[a + 3 : a + 4, :] + odd) * (1.0 / 64.0)
        out_ref[3 * a + 2 : 3 * a + 3, :] = (cosine[a : a + 1, :] - sine[a + 3 : a + 4, :] + odd) * (1.0 / 64.0)

    drain(go.at[0], pair_send)
    drain(r0, a_send.at[0])
    drain(r1, a_send.at[1])
    drain(u0, b_send.at[0])
    drain(u1, b_send.at[1])
    drain(zr, c_send)
    for n, ref in ((0, as_t), (1, as_g), (5, fs)):
        drain(ref.at[pl.ds(0, 120)], one_send.at[n])
    for n, ref in ((2, ks_t), (3, ks_g), (4, ao)):
        drain(ref.at[pl.ds(0, PLANE - 1)], one_send.at[n])
    drain(nr, one_send.at[6])


def body(inputs, cotangent, kernel_taps):
    vmem = lambda *shape: pltpu.VMEM(shape, F32)
    out = pl.pallas_call(
        kernel,
        out_shape=jax.ShapeDtypeStruct((9, 128), F32),
        in_specs=[pl.BlockSpec(memory_space=pltpu.VMEM)] * 3,
        out_specs=pl.BlockSpec(memory_space=pltpu.VMEM),
        scratch_shapes=[
            pltpu.VMEM((CHANNELS, CELLS), BF16),
            pltpu.VMEM((3, CELLS + 64, CHANNELS), BF16),
            vmem(2, 9, 4, 4, 2, 8, 128),
            vmem(9, 4, 4, 2, 8, 128),
            vmem(3, 4, 3, 4, 8, 128),
            vmem(3, 4, 3, 4, 8, 128),
            vmem(3, 3, 3, 4, 8, 128),
            vmem(3, 3, 3, 4, 8, 128),
            vmem(3, 4, 3, 8, 128),
            vmem(3, 4, 3, 8, 128),
            vmem(3, 3, 3, 8, 128),
            vmem(3, 3, 3, 8, 128),
            vmem(DEPTH, 9, 128),
            vmem(DEPTH - 1, 9, 128),
            vmem(9, 128),
            vmem(128, 128),
            vmem(128, 128),
            vmem(128, 128),
            vmem(128, 128),
            vmem(1, 128),
            vmem(PLANE - 1, 1, 128),
            vmem(PLANE, 32, 128),
            vmem(PLANE, 32, 128),
            vmem(PLANE, 32, 128),
            vmem(PLANE, 32, 128),
            vmem(2, 256, 256),
            vmem(PLANE, 32, 128),
            vmem(PLANE, 32, 128),
            vmem(128, 128),
            vmem(128, 128),
            pltpu.SemaphoreType.DMA,
            pltpu.SemaphoreType.DMA((9,)),
            pltpu.SemaphoreType.DMA((2,)),
            pltpu.SemaphoreType.DMA((6,)),
            pltpu.SemaphoreType.DMA((2,)),
            pltpu.SemaphoreType.DMA((6,)),
            pltpu.SemaphoreType.DMA,
            pltpu.SemaphoreType.DMA,
            pltpu.SemaphoreType.DMA((7,)),
            pltpu.SemaphoreType.DMA((7,)),
        ],
        compiler_params=pltpu.CompilerParams(collective_id=0, has_side_effects=True, vmem_limit_bytes=50 * 2**20),
        name="step",
    )(inputs.reshape(CELLS, CHANNELS), cotangent.reshape(CELLS, CHANNELS), kernel_taps.reshape(9, 128))
    return out.reshape(9, 4, 32)


def solution(mesh):
    torus = Mesh(mesh.devices.reshape(4, 8, 2, 2, 4), AXES)
    return jax.shard_map(
        body,
        mesh=torus,
        in_specs=(P(DP_INNER, None, None, None), P(DP_INNER, None, None, None), P(None, DP, INNER)),
        out_specs=P(None, DP, INNER),
        check_vma=False,
    )
```

time: 527 us -> 79.3 us (0.15); the launches traced: 518 us -> 79 us
  waiting for transfers between devices: 274 us -> 0 us
  blocking collectives: 111 us -> 0 us
  Pallas kernels: 0 us -> 75.4 us
  local copies, waits for them, and re-layouts: 67.2 us -> 3.57 us
  matrix products: 26.4 us -> 0 us
  between operations: 14.6 us -> 0.01 us
  starting transfers between devices: 14.2 us -> 0 us
  other arithmetic: 9.74 us -> 0 us
    all_gather x1 -> x0, waiting for transfers between devices: 114 us -> none  [body(): gathered = lax.all_gather(col_blocks, DP, axis=1, tiled=True)]
    reduce_scatter x2 -> x0, waiting for transfers between devices: 101 us -> none  [sum_in_order(): pieces = lax.psum_scatter(pieces, axes[k], scatter_dimension=0, tiled=True)]
    pallas_call x0 -> x1, Pallas kernels: none -> 75.4 us  [body(): pl.pallas_call(kernel, out_shape=jax.ShapeDtypeStruct((9, 128), F32), in_...]
    psum x5 -> x0, blocking collectives: 63.5 us -> none  [over_axes(): return functools.reduce(lax.psum, axes, value)]
    all_to_all x1 -> x0, waiting for transfers between devices: 58.3 us -> none  [one_exchange(): lax.all_to_all(pieces, axis, split_axis=0, concat_axis=0, tiled=True)]
    all_to_all x2 -> x0, blocking collectives: 47.9 us -> none  [the longest x1 26.3 us: summed_on_arrival(): lax.all_to_all(pieces, axis, split_axis=0, concat_axis=0, tiled=True)]
    dot_general x25 -> x0, matrix products: 26.4 us -> none  [the longest x16 17.6 us: matmul(): jnp.dot(left_side, right_side, precision=lax.Precision.HIGHEST, preferred...]
    dynamic_update_slice x8 -> x0, local copies, waits for them, and re-layouts: 15.2 us -> none  [body(): real_part, imag_part = lax.map(orthonormalize, (real_part, imag_part))]
  transfers between devices with their start and end apart: 4 -> 0, of which waited for: 4 -> 0; matrix products, arithmetic and copies ran while one was open for 0% -> 0% of each run, Pallas kernels for 0% -> 0%
where the time goes in v1:
time: 79.3 us; the launch traced here: 79 us
  Pallas kernels  75.4 us (95%)
  local copies, waits for them, and re-layouts  3.57 us (5%)
    pallas_call x1, Pallas kernels, body(): pl.pallas_call(kernel, out_shape=jax.ShapeDtypeStruct((9, 128), F32), in_...  75.4 us
    unnamed x4, local copies, waits for them, and re-layouts  2.08 us

profile of v1, /device:TPU:1, one launch (start us, length us, event | category | flops | bytes accessed | tf_op | source)
XLA Modules:
  0.0 79.0 jit_solution(13445376114471524495)
XLA Ops:
  0.0 0.8 %reshape.14.taps_ref = f32[9,128]{1,0:T(8,128)S(1)} reshape(f32[9,4,32]{2,1,0:T(4,128)} %param.5) | data formatting | bytes 9216 | tf_op jit(solution)/shard_map/reshape | solution.py:411
  0.8 0.0 copy-start
  0.8 1.0 %copy-done = bf16[1,32,32,256]{3,2,1,0:T(8,128)(2,1)S(1)} copy-done((bf16[1,32,32,256]{3,2,1,0:T(8,128)(2,1)S(1)}, bf16[1,32,32,256]{3,2,1,0:T(8,128)(2,1)}, u32[]{:S(2)}) %copy-start) | copy-done | bytes 524312
  1.8 0.0 copy-start.1
  1.8 1.0 %copy-done.1 = bf16[1,32,32,256]{3,2,1,0:T(8,128)(2,1)S(1)} copy-done((bf16[1,32,32,256]{3,2,1,0:T(8,128)(2,1)S(1)}, bf16[1,32,32,256]{3,2,1,0:T(8,128)(2,1)}, u32[]{:S(2)}) %copy-start.1) | copy-done | bytes 524312
  2.9 75.4 %step.1 = f32[9,128]{1,0:T(8,128)S(1)} custom-call(bf16[1024,256]{1,0:T(8,128)(2,1)S(1)} %bitcast.2, bf16[1024,256]{1,0:T(8,128)(2,1)S(1)} %bitcast.3, f32[9,128]{1,0:T(8,128)S(1)} %reshape.14.taps_ref), custom_call_target="tpu_custom_call" | custom-call | tf_op jit(solution)/shard_map/step/pallas_call | solution.py:362
  78.3 0.7 reshape.15
Async XLA Ops:
  0.8 1.0 %copy-start = (bf16[1,32,32,256]{3,2,1,0:T(8,128)(2,1)S(1)}, bf16[1,32,32,256]{3,2,1,0:T(8,128)(2,1)}, u32[]{:S(2)}) copy-start(bf16[1,32,32,256]{3,2,1,0:T(8,128)(2,1)} %param.3) | copy-start | bytes 1572868
  1.8 1.0 %copy-start.1 = (bf16[1,32,32,256]{3,2,1,0:T(8,128)(2,1)S(1)}, bf16[1,32,32,256]{3,2,1,0:T(8,128)(2,1)}, u32[]{:S(2)}) copy-start(bf16[1,32,32,256]{3,2,1,0:T(8,128)(2,1)} %param.4) | copy-start | bytes 1572868

commit v2 on v1

v2 whole, which is shorter than its diff:
```python
import functools
import math

import jax
import jax.numpy as jnp
from jax import lax
from jax.experimental import pallas as pl
from jax.experimental.pallas import tpu as pltpu
from jax.sharding import Mesh
from jax.sharding import PartitionSpec as P

AXES = ("dp_0", "dp_1", "dp_2", "inner_0", "inner_1")
INNER = ("inner_0", "inner_1")
DP = ("dp_0", "dp_1", "dp_2")
DP_INNER = DP + INNER
SIDE = 32
CHANNELS = 256
CELLS = SIDE * SIDE
STEP = 0.06 * math.sqrt(CHANNELS)
F32 = jnp.float32
BF16 = jnp.bfloat16
PLANE = 32
DEPTH = 16
CHUNKS = 3
MESH = pl.DeviceIdType.MESH
PEERS = sorted(
    [(dy, dc, dx) for dy in range(4) for dc in range(2) for dx in range(4) if dy or dc or dx],
    key=lambda m: -(min(m[0], 4 - m[0]) + min(m[2], 4 - m[2])),
)
STEPS = sorted(range(1, DEPTH), key=lambda d: -min(d, DEPTH - d))
COS = [math.cos(2.0 * math.pi * k / SIDE) for k in range(SIDE)]
SIN = [math.sin(2.0 * math.pi * k / SIDE) for k in range(SIDE)]


def swap_groups(parts):
    lane = lax.broadcasted_iota(jnp.int32, parts[0].shape, 1)
    low = lane < 64
    even = (lane & 32) == 0
    v0, v1, v2, v3 = parts
    w0 = jnp.where(low, v0, pltpu.roll(v2, 64, 1))
    w2 = jnp.where(low, pltpu.roll(v0, 64, 1), v2)
    w1 = jnp.where(low, v1, pltpu.roll(v3, 64, 1))
    w3 = jnp.where(low, pltpu.roll(v1, 64, 1), v3)
    u0 = jnp.where(even, w0, pltpu.roll(w1, 32, 1))
    u1 = jnp.where(even, pltpu.roll(w0, 96, 1), w1)
    u2 = jnp.where(even, w2, pltpu.roll(w3, 32, 1))
    u3 = jnp.where(even, pltpu.roll(w2, 96, 1), w3)
    return u0, u1, u2, u3


def halves(value):
    high = value.astype(BF16)
    low = (value - high.astype(F32)).astype(BF16)
    return high, low


def product(left, right):
    dot = functools.partial(jnp.dot, preferred_element_type=F32)
    return dot(left[0], right[0]) + (dot(left[0], right[1]) + dot(left[1], right[0]))


def kernel(x_hbm, ct_hbm, taps_hbm, out_ref, x_ref, ct_ref, taps_ref, xt, cb, go, gr, s0, s1, r0, r1, t0, t1, u0, u1, zs, zr, gs, as_t, ar_t,
           as_g, ar_g, nv, nr, ks_t, kr_t, ks_g, kr_g, mat, ao, ar, fs, fr, pair_send, pair_recv, a_send, a_recv,
           b_send, b_recv, c_send, c_recv, one_send, one_recv, load_sem):
    y = lax.axis_index("dp_0")
    zl = lax.axis_index("dp_1")
    c = lax.axis_index("dp_2")
    zh = lax.axis_index("inner_0")
    x = lax.axis_index("inner_1")
    z = zh * 8 + zl
    p = (y * 2 + c) * 4 + x

    ys = [y] + [lax.rem(y + d, 4) for d in range(1, 4)]
    xs = [x] + [lax.rem(x + d, 4) for d in range(1, 4)]
    cores = [c, 1 - c]
    depths = [z] + [lax.rem(z + d, DEPTH) for d in range(1, DEPTH)]

    def at_plane(peer):
        dy, dc, dx = peer
        return (ys[dy], zl, cores[dc], zh, xs[dx])

    def place(peer):
        dy, dc, dx = peer
        return (ys[dy] * 2 + cores[dc]) * 4 + xs[dx]

    def at_depth(d):
        return (y, lax.rem(depths[d], 8), c, lax.div(depths[d], 8), x)

    def send(src, dst, send_sem, recv_sem, device):
        pltpu.make_async_remote_copy(
            src_ref=src, dst_ref=dst, send_sem=send_sem, recv_sem=recv_sem, device_id=device, device_id_type=MESH
        ).start()

    def drain(ref, sem):
        pltpu.make_async_copy(ref, ref, sem).wait()

    pending = []

    def finish():
        for ref, sem in pending:
            drain(ref, sem)

    loads = [
        pltpu.make_async_copy(src, dst, load_sem.at[n])
        for n, (src, dst) in enumerate(((x_hbm, x_ref), (ct_hbm, ct_ref), (taps_hbm, taps_ref)))
    ]
    for load in loads:
        load.start()
    barrier = pltpu.get_barrier_semaphore()
    for d in STEPS:
        pl.semaphore_signal(barrier, inc=1, device_id=at_depth(d), device_id_type=MESH)
    for peer in PEERS:
        pl.semaphore_signal(barrier, inc=1, device_id=at_plane(peer), device_id_type=MESH)

    row = lax.broadcasted_iota(jnp.int32, (256, 256), 0)
    col = lax.broadcasted_iota(jnp.int32, (256, 256), 1)
    channel = (row & 192) + (row & 7) * 8 + ((row >> 5) & 1) * 4 + ((row >> 3) & 3)
    order = jnp.where(col == channel, 1.0, 0.0).astype(BF16)
    loads[0].wait()
    for k in range(4):
        xt[:, k * 256 : (k + 1) * 256] = lax.dot_general(
            order, x_ref[k * 256 : (k + 1) * 256, :], (((1,), (1,)), ((), ())), preferred_element_type=F32
        ).astype(BF16)
    loads[1].wait()
    for m in range(3):
        source = (row & 224) + ((row + (33 - m)) & 31)
        shift = jnp.where(col == source, 1.0, 0.0).astype(BF16)
        for k in range(4):
            rows = ct_ref[k * 256 : (k + 1) * 256, :]
            if m != 1:
                rows = jnp.dot(shift, rows, preferred_element_type=F32).astype(BF16)
            cb[m, 32 + k * 256 : 32 + (k + 1) * 256, :] = rows
        cb[m, 0:32, :] = cb[m, 1024:1056, :]
        cb[m, 1056:1088, :] = cb[m, 32:64, :]

    def depth_messages(block, dst):
        before, middle, after = [
            jnp.concatenate([block[3 * a + b : 3 * a + b + 1, :] for a in range(3)], axis=0) for b in range(3)
        ]
        both = after + before
        apart = after - before
        for w in range(DEPTH):
            if w == 0:
                upper, lower = middle + both, middle - both
            else:
                upper, lower = middle + COS[w] * both, -SIN[w] * apart
            dst[8 * w : 8 * w + 3, :] = upper
            dst[8 * w + 3 : 8 * w + 6, :] = lower
        return None

    def depth_send(src, dst, sem):
        for d in STEPS:
            slot = (4 - d) % DEPTH
            send(src.at[pl.ds(pl.multiple_of(depths[d] * 8, 8), 8)], dst.at[pl.ds(8 * slot, 8)],
                 one_send.at[sem], one_recv.at[sem + slot // 8], at_depth(d))
        dst[32:40, :] = src[pl.ds(pl.multiple_of(z * 8, 8), 8), :]
        pending.append((src.at[pl.ds(0, 120)], one_send.at[sem]))

    def depth_wait(dst, sem, half):
        drain(dst.at[pl.ds(0, 64 if half else 56)], one_recv.at[sem + half])

    def plane_messages(src, dst, half):
        parts = [src[pl.ds(64 * half + m, 8, stride=8), :] for m in range(6)]

        @pl.when(z != 0)
        def _():
            real_sum, real_gap = parts[2] + parts[0], parts[2] - parts[0]
            imag_sum, imag_gap = parts[5] + parts[3], parts[5] - parts[3]
            for k in range(17):
                upper, upper_gap = parts[1] + COS[k] * real_sum, SIN[k] * imag_gap
                lower, lower_gap = parts[4] + COS[k] * imag_sum, SIN[k] * real_gap
                dst[half, k, 0] = upper + upper_gap
                dst[half, k, 1] = lower - lower_gap
                if 0 < k < 16:
                    dst[half, 32 - k, 0] = upper - upper_gap
                    dst[half, 32 - k, 1] = lower + lower_gap

        @pl.when(z == 0)
        def _():
            for edge in range(2):
                first, mid, last = parts[3 * edge : 3 * edge + 3]
                total, gap = last + first, last - first
                dst[half, 16 * edge, 0] = mid + total
                dst[half, 16 * edge, 1] = mid - total
                for k in range(1, 16):
                    dst[half, 16 * edge + k, 0] = mid + COS[k] * total
                    dst[half, 16 * edge + k, 1] = -SIN[k] * gap

    def plane_send(src, dst, half, sem):
        for peer in PEERS:
            send(src.at[half, place(peer)], dst.at[half, p], one_send.at[sem + half], one_recv.at[sem + half], at_plane(peer))
        dst[half, p] = src[half, p]
        pending.append((src.at[half, pl.ds(0, PLANE - 1)], one_send.at[sem + half]))

    def plane_wait(dst, half, sem):
        drain(dst.at[half, pl.ds(0, PLANE - 1)], one_recv.at[sem + half])

    sublane = lax.broadcasted_iota(jnp.int32, (8, 128), 0)

    def turned(low, high, shift):
        rest = lax.rem(shift, 8)
        kept = (sublane >= rest) == (shift < 8)
        low, high = pltpu.roll(low, rest, 0), pltpu.roll(high, rest, 0)
        return jnp.where(kept, low, high), jnp.where(kept, high, low)

    as_t[...] = jnp.zeros_like(as_t)
    as_g[...] = jnp.zeros_like(as_g)
    fs[...] = jnp.zeros_like(fs)
    loads[2].wait()
    depth_messages(jnp.concatenate([taps_ref[:, i, :] for i in range(4)], axis=1), as_t)

    def chunk_out(ch):
        for t in range(3):
            drain(gr.at[3 * ch + t], pair_recv.at[3 * ch + t])
        for t in range(3):
            for yy in range(4):
                for xx in range(4):
                    s0[ch, xx, t, yy] = go[c, 3 * ch + t, yy, xx, 0] + gr[3 * ch + t, yy, xx, 0]
                    s1[ch, yy, t, xx] = go[c, 3 * ch + t, yy, xx, 1] + gr[3 * ch + t, yy, xx, 1]
        for d in (1, 3, 2):
            xx, yy = xs[d], ys[d]
            send(s0.at[ch, xx], r0.at[ch, d - 1], a_send.at[0], a_recv.at[ch], (y, zl, c, zh, xx))
            send(s1.at[ch, yy], r1.at[ch, d - 1], a_send.at[1], a_recv.at[3 + ch], (yy, zl, c, zh, x))

    def chunk_on(ch):
        drain(r0.at[ch], a_recv.at[ch])
        for t in range(3):
            for yy in range(4):
                t0[ch, yy, t] = (s0[ch, x, t, yy] + r0[ch, 0, t, yy]) + (r0[ch, 1, t, yy] + r0[ch, 2, t, yy])
        for d in (1, 3, 2):
            yy = ys[d]
            send(t0.at[ch, yy], u0.at[ch, d - 1], b_send.at[0], b_recv.at[ch], (yy, zl, c, zh, x))
        drain(r1.at[ch], a_recv.at[3 + ch])
        for t in range(3):
            for xx in range(4):
                t1[ch, xx, t] = (s1[ch, y, t, xx] + r1[ch, 0, t, xx]) + (r1[ch, 1, t, xx] + r1[ch, 2, t, xx])
        for d in (1, 3, 2):
            xx = xs[d]
            send(t1.at[ch, xx], u1.at[ch, d - 1], b_send.at[1], b_recv.at[3 + ch], (y, zl, c, zh, xx))

    def chunk_in(ch):
        drain(u0.at[ch], b_recv.at[ch])
        drain(u1.at[ch], b_recv.at[3 + ch])
        for t in range(3):
            first = (t0[ch, y, t] + u0[ch, 0, t]) + (u0[ch, 1, t] + u0[ch, 2, t])
            second = (t1[ch, x, t] + u1[ch, 0, t]) + (u1[ch, 1, t] + u1[ch, 2, t])
            for w in range(8):
                zs[w, 3 * ch + t : 3 * ch + t + 1, :] = first[w : w + 1, :]
                zs[8 + w, 3 * ch + t : 3 * ch + t + 1, :] = second[w : w + 1, :]

    for t in range(9):
        a, b = t // 3 - 1, t % 3
        grad = jnp.dot(xt[...], cb[b, 32 - 32 * a : 32 - 32 * a + CELLS, :], preferred_element_type=F32)
        for yc in range(8):
            for h in range(2):
                parts = [grad[yc * 32 + i * 8 : yc * 32 + i * 8 + 8, h * 128 : h * 128 + 128] for i in range(4)]
                for xx, part in enumerate(swap_groups(parts)):
                    go[yc % 2, t, yc // 2, xx, h] = part
        if t == 0:
            pl.semaphore_wait(barrier, PLANE + DEPTH - 2)
            depth_send(as_t, ar_t, 0)
        send(go.at[1 - c, t], gr.at[t], pair_send, pair_recv.at[t], (y, zl, 1 - c, zh, x))
        if t == 4:
            chunk_out(0)
        if t == 7:
            chunk_out(1)
    chunk_out(2)
    pending.append((go.at[0], pair_send))
    pending.append((r0, a_send.at[0]))
    pending.append((r1, a_send.at[1]))
    for ch in range(CHUNKS):
        chunk_on(ch)
    pending.append((u0, b_send.at[0]))
    pending.append((u1, b_send.at[1]))
    for half in range(2):
        depth_wait(ar_t, 0, half)
        plane_messages(ar_t, ks_t, half)
        plane_send(ks_t, kr_t, half, 4)
    for ch in range(CHUNKS):
        chunk_in(ch)
    for d in STEPS:
        send(zs.at[depths[d]], zr.at[d - 1], c_send, c_recv, at_depth(d))
    drain(zr, c_recv)
    pending.append((zr, c_send))
    block = zs[z]
    for d in range(DEPTH - 1):
        block = block + zr[d]
    gs[...] = block
    depth_messages(gs[...], as_g)
    squares = jnp.sum(block * block, axis=0, keepdims=True)
    for w in range(DEPTH):
        as_g[8 * w + 6 : 8 * w + 7, :] = squares
    depth_send(as_g, ar_g, 2)
    depth_wait(ar_g, 2, 0)
    plane_messages(ar_g, ks_g, 0)
    plane_send(ks_g, kr_g, 0, 6)
    depth_wait(ar_g, 2, 1)
    plane_messages(ar_g, ks_g, 1)
    plane_send(ks_g, kr_g, 1, 6)
    nv[...] = jnp.sum(ar_g[pl.ds(6, DEPTH, stride=8), :], axis=0, keepdims=True)
    for d, peer in enumerate(PEERS):
        send(nv, nr.at[d], one_send.at[12], one_recv.at[12], at_plane(peer))
    pending.append((nr, one_send.at[12]))
    for half in range(2):
        plane_wait(kr_t, half, 4)
    drain(nr, one_recv.at[12])
    total = nv[...]
    for d in range(PLANE - 1):
        total = total + nr[d]
    norm = jnp.sqrt(jnp.sum(total, axis=1, keepdims=True))
    factor = jnp.broadcast_to(STEP / (norm + 1e-6), (8, 128))
    for half in range(2):
        plane_wait(kr_g, half, 6)

    onward = depths[12]
    for yc in range(8):
        for m in range(2):
            parts = []
            for xx in range(4):
                near, far = [kr_t[n, yc * 4 + xx, m] - factor * kr_g[n, yc * 4 + xx, m] for n in range(2)]
                parts.append(turned(near, far, onward))
            for h in range(2):
                for i, part in enumerate(swap_groups([pair[h] for pair in parts])):
                    mat[m, yc * 32 + i * 8 : yc * 32 + i * 8 + 8, h * 128 : h * 128 + 128] = part

    joint = jnp.where((z == 0) & (p % 16 == 0), 0.0, 1.0).astype(F32)
    for _ in range(2):
        real, imag = mat[0], mat[1]
        real_2, imag_2 = halves(real), halves(imag)
        real_t, imag_t = halves(real.T), halves(imag.T)
        first = product(real_t, real_2)
        second = product(imag_t, imag_2)
        cross = product(real_t, imag_2) - product(imag_t, real_2)
        eye = jnp.where(row == col, 1.5, 0.0)
        mix_first = halves(eye - 0.5 * (first + joint * second))
        mix_second = halves(eye - 0.5 * (second + joint * first))
        mix_cross = halves((-0.5 * joint) * cross)
        mat[0] = product(real_2, mix_first) - product(imag_2, mix_cross)
        mat[1] = product(real_2, mix_cross) + product(imag_2, mix_second)

    back = lax.rem(20 - z, DEPTH)
    for yc in range(8):
        for m in range(2):
            low, high = [
                swap_groups(
                    [mat[m, yc * 32 + i * 8 : yc * 32 + i * 8 + 8, h * 128 : h * 128 + 128] for i in range(4)]
                )
                for h in range(2)
            ]
            for xx in range(4):
                ao[0, yc * 4 + xx, m], ao[1, yc * 4 + xx, m] = turned(low[xx], high[xx], back)
    plane_send(ao, ar, 1, 8)
    plane_send(ao, ar, 0, 8)

    def summed(half, first, last, base):
        real_0 = imag_0 = real_c = real_s = imag_c = imag_s = jnp.zeros((8, 128), F32)
        for k in range(first, last):
            real, imag = ar[half, k, 0], ar[half, k, 1]
            ck, sk = COS[k - base], SIN[k - base]
            real_0, imag_0 = real_0 + real, imag_0 + imag
            real_c, real_s = real_c + ck * real, real_s + sk * real
            imag_c, imag_s = imag_c + ck * imag, imag_s + sk * imag
        return real_0, imag_0, real_c, real_s, imag_c, imag_s

    for half in (1, 0):
        plane_wait(ar, half, 8)

        @pl.when(z != 0)
        def _():
            real_0, imag_0, real_c, real_s, imag_c, imag_s = summed(half, 0, 32, 0)
            parts = (real_c + imag_s, real_0, real_c - imag_s, imag_c - real_s, imag_0, imag_c + real_s)
            for m, part in enumerate(parts):
                fs[pl.ds(64 * half + m, 8, stride=8), :] = 2.0 * part

        @pl.when(z == 0)
        def _():
            for edge in range(2):
                base = 16 * edge
                real_0, imag_0, real_c, real_s, imag_c, imag_s = summed(half, base + 1, base + 16, base)
                one, other = ar[half, base, 0], ar[half, base, 1]
                parts = (
                    2.0 * (real_c + imag_s) + (one - other),
                    2.0 * real_0 + (one + other),
                    2.0 * (real_c - imag_s) + (one - other),
                )
                for m, part in enumerate(parts):
                    fs[pl.ds(64 * half + 3 * edge + m, 8, stride=8), :] = part

        own = pl.ds(pl.multiple_of(z * 8, 8), 8)
        for d in STEPS:
            slot = (d + 4) % DEPTH
            if slot // 8 == half:
                send(fs.at[pl.ds(8 * slot, 8)], fr.at[own], one_send.at[10], one_recv.at[10], at_depth(d))
        if half == 0:
            fr[own, :] = fs[32:40, :]
    pending.append((fs.at[pl.ds(0, 120)], one_send.at[10]))
    drain(fr.at[pl.ds(0, 120)], one_recv.at[10])
    plain = fr[8:16, :]
    cosine = COS[1] * fr[8:16, :]
    sine = SIN[1] * fr[8:16, :]
    for w in range(2, DEPTH):
        tile = fr[8 * w : 8 * w + 8, :]
        plain, cosine, sine = plain + tile, cosine + COS[w] * tile, sine + SIN[w] * tile
    edge = fr[0:8, :]
    for a in range(3):
        first, last = edge[a : a + 1, :], edge[a + 3 : a + 4, :]
        even, odd = first + last, first - last
        out_ref[3 * a + 1 : 3 * a + 2, :] = (plain[a : a + 1, :] + even) * (1.0 / 64.0)
        out_ref[3 * a : 3 * a + 1, :] = (cosine[a : a + 1, :] + sine[a + 3 : a + 4, :] + odd) * (1.0 / 64.0)
        out_ref[3 * a + 2 : 3 * a + 3, :] = (cosine[a : a + 1, :] - sine[a + 3 : a + 4, :] + odd) * (1.0 / 64.0)

    finish()


def body(inputs, cotangent, kernel_taps):
    vmem = lambda *shape: pltpu.VMEM(shape, F32)
    out = pl.pallas_call(
        kernel,
        out_shape=jax.ShapeDtypeStruct((9, 128), F32),
        in_specs=[pl.BlockSpec(memory_space=pl.ANY)] * 3,
        out_specs=pl.BlockSpec(memory_space=pltpu.VMEM),
        scratch_shapes=[
            pltpu.VMEM((CELLS, CHANNELS), BF16),
            pltpu.VMEM((CELLS, CHANNELS), BF16),
            vmem(9, 4, 32),
            pltpu.VMEM((CHANNELS, CELLS), BF16),
            pltpu.VMEM((3, CELLS + 64, CHANNELS), BF16),
            vmem(2, 9, 4, 4, 2, 8, 128),
            vmem(9, 4, 4, 2, 8, 128),
            vmem(3, 4, 3, 4, 8, 128),
            vmem(3, 4, 3, 4, 8, 128),
            vmem(3, 3, 3, 4, 8, 128),
            vmem(3, 3, 3, 4, 8, 128),
            vmem(3, 4, 3, 8, 128),
            vmem(3, 4, 3, 8, 128),
            vmem(3, 3, 3, 8, 128),
            vmem(3, 3, 3, 8, 128),
            vmem(DEPTH, 9, 128),
            vmem(DEPTH - 1, 9, 128),
            vmem(9, 128),
            vmem(128, 128),
            vmem(128, 128),
            vmem(128, 128),
            vmem(128, 128),
            vmem(1, 128),
            vmem(PLANE - 1, 1, 128),
            vmem(2, PLANE, 2, 8, 128),
            vmem(2, PLANE, 2, 8, 128),
            vmem(2, PLANE, 2, 8, 128),
            vmem(2, PLANE, 2, 8, 128),
            vmem(2, 256, 256),
            vmem(2, PLANE, 2, 8, 128),
            vmem(2, PLANE, 2, 8, 128),
            vmem(128, 128),
            vmem(128, 128),
            pltpu.SemaphoreType.DMA,
            pltpu.SemaphoreType.DMA((9,)),
            pltpu.SemaphoreType.DMA((2,)),
            pltpu.SemaphoreType.DMA((6,)),
            pltpu.SemaphoreType.DMA((2,)),
            pltpu.SemaphoreType.DMA((6,)),
            pltpu.SemaphoreType.DMA,
            pltpu.SemaphoreType.DMA,
            pltpu.SemaphoreType.DMA((13,)),
            pltpu.SemaphoreType.DMA((13,)),
            pltpu.SemaphoreType.DMA((3,)),
        ],
        compiler_params=pltpu.CompilerParams(collective_id=0, has_side_effects=True, vmem_limit_bytes=63 * 2**20),
        name="step",
    )(inputs.reshape(CELLS, CHANNELS), cotangent.reshape(CELLS, CHANNELS), kernel_taps)
    return out.reshape(9, 4, 32)


def solution(mesh):
    torus = Mesh(mesh.devices.reshape(4, 8, 2, 2, 4), AXES)
    return jax.shard_map(
        body,
        mesh=torus,
        in_specs=(P(DP_INNER, None, None, None), P(DP_INNER, None, None, None), P(None, DP, INNER)),
        out_specs=P(None, DP, INNER),
        check_vma=False,
    )
```

time: 79.3 us -> 72.5 us (0.914)
  Pallas kernels: 75.4 us -> 70.9 us
  local copies, waits for them, and re-layouts: 3.57 us -> 1.38 us
    pallas_call x1, Pallas kernels: 75.4 us -> 70.9 us  [body(): pl.pallas_call(kernel, out_shape=jax.ShapeDtypeStruct((9, 128), F32), in_...]
    unnamed x4 -> x0, local copies, waits for them, and re-layouts: 2.08 us -> none
    reshape x1 -> x0, local copies, waits for them, and re-layouts: 0.8 us -> none  [body(): kernel_taps.reshape(9, 128)]
where the time goes in v2:
time: 72.5 us; the launch traced here: 72.3 us
  Pallas kernels  70.9 us (98%)
  local copies, waits for them, and re-layouts  1.38 us (2%)
    pallas_call x1, Pallas kernels, body(): pl.pallas_call(kernel, out_shape=jax.ShapeDtypeStruct((9, 128), F32), in_...  70.9 us

profile of v2, /device:TPU:1, one launch (start us, length us, event | category | flops | bytes accessed | tf_op | source)
XLA Modules:
  0.0 72.3 jit_solution(3134623127021135330)
XLA Ops:
  0.0 70.9 %step.1 = f32[9,128]{1,0:T(8,128)} custom-call(bf16[1024,256]{1,0:T(8,128)(2,1)} %bitcast.2, bf16[1024,256]{1,0:T(8,128)(2,1)} %bitcast.3, f32[9,4,32]{2,1,0:T(4,128)} %taps_hbm.1), custom_call_target="tpu_custom_call" | custom-call | tf_op jit(solution)/shard_map/step/pallas_call | solution.py:417
  70.9 1.4 %reshape.11 = f32[9,4,32]{2,1,0:T(4,128)} reshape(f32[9,128]{1,0:T(8,128)} %step.1) | data formatting | bytes 9216 | tf_op jit(solution)/shard_map/reshape | solution.py:471

commit v3 on v2

--- a/solution.py
+++ b/solution.py
@@ -61,7 +61,7 @@
 
 def kernel(x_hbm, ct_hbm, taps_hbm, out_ref, x_ref, ct_ref, taps_ref, xt, cb, go, gr, s0, s1, r0, r1, t0, t1, u0, u1, zs, zr, gs, as_t, ar_t,
            as_g, ar_g, nv, nr, ks_t, kr_t, ks_g, kr_g, mat, ao, ar, fs, fr, pair_send, pair_recv, a_send, a_recv,
-           b_send, b_recv, c_send, c_recv, one_send, one_recv, load_sem):
+           b_send, b_recv, c_send, c_recv, one_send, one_recv, load_sem, known):
     y = lax.axis_index("dp_0")
     zl = lax.axis_index("dp_1")
     c = lax.axis_index("dp_2")
@@ -107,10 +107,21 @@
     for load in loads:
         load.start()
     barrier = pltpu.get_barrier_semaphore()
-    for d in STEPS:
+    lines = [peer for peer in PEERS if sum(step != 0 for step in peer) == 1]
+    for peer in lines:
+        pl.semaphore_signal(barrier, inc=1, device_id=at_plane(peer), device_id_type=MESH)
+    for d in (1, DEPTH - 1):
         pl.semaphore_signal(barrier, inc=1, device_id=at_depth(d), device_id_type=MESH)
-    for peer in PEERS:
-        pl.semaphore_signal(barrier, inc=1, device_id=at_plane(peer), device_id_type=MESH)
+
+    def tell(stage):
+        for d in (2**stage, DEPTH - 2**stage):
+            pl.semaphore_signal(known.at[stage], inc=1, device_id=at_depth(d), device_id_type=MESH)
+
+    def learn(stage):
+        pl.semaphore_wait(known.at[stage], 2)
+        if stage < 2:
+            tell(stage + 1)
+
 
     row = lax.broadcasted_iota(jnp.int32, (256, 256), 0)
     col = lax.broadcasted_iota(jnp.int32, (256, 256), 1)
@@ -257,29 +268,34 @@
                 for xx, part in enumerate(swap_groups(parts)):
                     go[yc % 2, t, yc // 2, xx, h] = part
         if t == 0:
-            pl.semaphore_wait(barrier, PLANE + DEPTH - 2)
-            depth_send(as_t, ar_t, 0)
+            pl.semaphore_wait(barrier, len(lines) + 2)
+            tell(0)
         send(go.at[1 - c, t], gr.at[t], pair_send, pair_recv.at[t], (y, zl, 1 - c, zh, x))
         if t == 4:
             chunk_out(0)
         if t == 7:
             chunk_out(1)
+            learn(0)
     chunk_out(2)
     pending.append((go.at[0], pair_send))
     pending.append((r0, a_send.at[0]))
     pending.append((r1, a_send.at[1]))
+    learn(1)
     for ch in range(CHUNKS):
         chunk_on(ch)
     pending.append((u0, b_send.at[0]))
     pending.append((u1, b_send.at[1]))
+    learn(2)
+    depth_send(as_t, ar_t, 0)
+    for ch in range(CHUNKS):
+        chunk_in(ch)
+
+    for d in STEPS:
+        send(zs.at[depths[d]], zr.at[d - 1], c_send, c_recv, at_depth(d))
     for half in range(2):
         depth_wait(ar_t, 0, half)
         plane_messages(ar_t, ks_t, half)
         plane_send(ks_t, kr_t, half, 4)
-    for ch in range(CHUNKS):
-        chunk_in(ch)
-    for d in STEPS:
-        send(zs.at[depths[d]], zr.at[d - 1], c_send, c_recv, at_depth(d))
     drain(zr, c_recv)
     pending.append((zr, c_send))
     block = zs[z]
@@ -464,6 +480,7 @@
             pltpu.SemaphoreType.DMA((13,)),
             pltpu.SemaphoreType.DMA((13,)),
             pltpu.SemaphoreType.DMA((3,)),
+            pltpu.SemaphoreType.REGULAR((3,)),
         ],
         compiler_params=pltpu.CompilerParams(collective_id=0, has_side_effects=True, vmem_limit_bytes=63 * 2**20),
         name="step",

time: 72.5 us -> 68.7 us (0.948)
  Pallas kernels: 70.9 us -> 67.1 us
    pallas_call x1, Pallas kernels: 70.9 us -> 67.1 us  [body(): pl.pallas_call(kernel, out_shape=jax.ShapeDtypeStruct((9, 128), F32), in_...]
where the time goes in v3:
time: 68.7 us; the launch traced here: 68.5 us
  Pallas kernels  67.1 us (98%)
  local copies, waits for them, and re-layouts  1.38 us (2%)
    pallas_call x1, Pallas kernels, body(): pl.pallas_call(kernel, out_shape=jax.ShapeDtypeStruct((9, 128), F32), in_...  67.1 us
    reshape x1, local copies, waits for them, and re-layouts, body(): return out.reshape(9, 4, 32)  1.38 us

profile of v3, /device:TPU:1, one launch (start us, length us, event | category | flops | bytes accessed | tf_op | source)
XLA Modules:
  0.0 68.5 jit_solution(15100305828428076492)
XLA Ops:
  0.0 67.1 %step.1 = f32[9,128]{1,0:T(8,128)} custom-call(bf16[1024,256]{1,0:T(8,128)(2,1)} %bitcast.2, bf16[1024,256]{1,0:T(8,128)(2,1)} %bitcast.3, f32[9,4,32]{2,1,0:T(4,128)} %taps_hbm.1), custom_call_target="tpu_custom_call" | custom-call | tf_op jit(solution)/shard_map/step/pallas_call | solution.py:433
  67.1 1.4 %reshape.11 = f32[9,4,32]{2,1,0:T(4,128)} reshape(f32[9,128]{1,0:T(8,128)} %step.1) | data formatting | bytes 9216 | tf_op jit(solution)/shard_map/reshape | solution.py:488

commit v4 on v3

--- a/solution.py
+++ b/solution.py
@@ -21,7 +21,9 @@
 BF16 = jnp.bfloat16
 PLANE = 32
 DEPTH = 16
-CHUNKS = 3
+TAPS = (1, 4, 7, 0, 3, 6, 2, 5, 8)
+GROUPS = ((0,), (1, 2), (3, 4, 5), (6, 7, 8))
+FLOWS = (("x", 1, (0, 2, 4, 6, 8)), ("y", 1, (1, 3, 5, 7)), ("x", 0, (1, 3, 5, 7)), ("y", 0, (0, 2, 4, 6, 8)))
 MESH = pl.DeviceIdType.MESH
 PEERS = sorted(
     [(dy, dc, dx) for dy in range(4) for dc in range(2) for dx in range(4) if dy or dc or dx],
@@ -59,7 +61,7 @@
     return dot(left[0], right[0]) + (dot(left[0], right[1]) + dot(left[1], right[0]))
 
 
-def kernel(x_hbm, ct_hbm, taps_hbm, out_ref, x_ref, ct_ref, taps_ref, xt, cb, go, gr, s0, s1, r0, r1, t0, t1, u0, u1, zs, zr, gs, as_t, ar_t,
+def kernel(x_hbm, ct_hbm, taps_hbm, out_ref, x_ref, ct_ref, taps_ref, xt, cb, go, gr, s0, s1, s2, s3, r0, r1, r2, r3, t0, t1, t2, t3, u0, u1, u2, u3, zs, zr, gs, as_t, ar_t,
            as_g, ar_g, nv, nr, ks_t, kr_t, ks_g, kr_g, mat, ao, ar, fs, fr, pair_send, pair_recv, a_send, a_recv,
            b_send, b_recv, c_send, c_recv, one_send, one_recv, load_sem, known):
     y = lax.axis_index("dp_0")
@@ -133,7 +135,8 @@
             order, x_ref[k * 256 : (k + 1) * 256, :], (((1,), (1,)), ((), ())), preferred_element_type=F32
         ).astype(BF16)
     loads[1].wait()
-    for m in range(3):
+
+    def moved(m):
         source = (row & 224) + ((row + (33 - m)) & 31)
         shift = jnp.where(col == source, 1.0, 0.0).astype(BF16)
         for k in range(4):
@@ -214,91 +217,118 @@
         low, high = pltpu.roll(low, rest, 0), pltpu.roll(high, rest, 0)
         return jnp.where(kept, low, high), jnp.where(kept, high, low)
 
+    sums, heard, lines_2, heard_2 = (s0, s1, s2, s3), (r0, r1, r2, r3), (t0, t1, t2, t3), (u0, u1, u2, u3)
+    along = {"x": (xs, lambda v: (y, zl, c, zh, v)), "y": (ys, lambda v: (v, zl, c, zh, x))}
+
+    def chunk_out(ch):
+        for n in GROUPS[ch]:
+            drain(gr.at[n], pair_recv.at[n])
+        for f, (axis, half, places) in enumerate(FLOWS):
+            ready = [k for k, n in enumerate(places) if n in GROUPS[ch]]
+            for k in ready:
+                n = places[k]
+                for yy in range(4):
+                    for xx in range(4):
+                        to, other = (xx, yy) if axis == "x" else (yy, xx)
+                        sums[f][to, k, other] = go[c, n, yy, xx, half] + gr[n, yy, xx, half]
+            if ready and (half or ch == 0):
+                flow_out(f, ready[0], len(ready))
+
+    def flow_out(f, start, count):
+        where, device = along[FLOWS[f][0]]
+        part = pl.ds(start, count)
+        for d in (2, 1, 3):
+            send(sums[f].at[where[d], part], heard[f].at[d - 1, part], a_send.at[f], a_recv.at[f], device(where[d]))
+
+    def flow_on(f):
+        axis, _, places = FLOWS[f]
+        mine = x if axis == "x" else y
+        where, device = along["y" if axis == "x" else "x"]
+        drain(heard[f], a_recv.at[f])
+        for k in range(len(places)):
+            for o in range(4):
+                lines_2[f][o, k] = (sums[f][mine, k, o] + heard[f][0, k, o]) + (heard[f][1, k, o] + heard[f][2, k, o])
+        for d in (2, 1, 3):
+            send(lines_2[f].at[where[d]], heard_2[f].at[d - 1], b_send.at[f], b_recv.at[f], device(where[d]))
+        pending.append((heard[f], a_send.at[f]))
+        pending.append((heard_2[f], b_send.at[f]))
+
+    def flow_in(f):
+        axis, half, places = FLOWS[f]
+        mine = y if axis == "x" else x
+        drain(heard_2[f], b_recv.at[f])
+        for k, n in enumerate(places):
+            tile = (lines_2[f][mine, k] + heard_2[f][0, k]) + (heard_2[f][1, k] + heard_2[f][2, k])
+            for w in range(8):
+                zs[8 * half + w, TAPS[n] : TAPS[n] + 1, :] = tile[w : w + 1, :]
+
+    def depth_sum(half):
+        for d in STEPS:
+            slot = (d + 4) % DEPTH
+            if slot // 8 == half:
+                send(zs.at[slot], zr.at[d - 1], c_send, c_recv, at_depth(d))
+
+    back = lax.rem(20 - z, DEPTH)
+    moved(1)
+    for n, t in enumerate(TAPS):
+        a, b = t // 3 - 1, t % 3
+        grad = jnp.dot(xt[...], cb[b, 32 - 32 * a : 32 - 32 * a + CELLS, :], preferred_element_type=F32)
+        for yc in range(8):
+            low, high = [
+                swap_groups(
+                    [grad[yc * 32 + i * 8 : yc * 32 + i * 8 + 8, h * 128 : h * 128 + 128] for i in range(4)]
+                )
+                for h in range(2)
+            ]
+            for xx in range(4):
+                near, far = turned(low[xx], high[xx], back)
+                go[yc % 2, n, yc // 2, xx, 0] = near
+                go[yc % 2, n, yc // 2, xx, 1] = far
+        if n == 0:
+            pl.semaphore_wait(barrier, len(lines) + 2)
+            tell(0)
+        send(go.at[1 - c, n], gr.at[n], pair_send, pair_recv.at[n], (y, zl, 1 - c, zh, x))
+        if n == 2:
+            moved(0)
+            chunk_out(0)
+        if n == 3:
+            chunk_out(1)
+        if n == 5:
+            moved(2)
+        if n == 6:
+            chunk_out(2)
+            learn(0)
+    chunk_out(3)
+    flow_out(2, 0, 4)
+    flow_out(3, 1, 4)
+    pending.append((go.at[0], pair_send))
     as_t[...] = jnp.zeros_like(as_t)
     as_g[...] = jnp.zeros_like(as_g)
     fs[...] = jnp.zeros_like(fs)
     loads[2].wait()
     depth_messages(jnp.concatenate([taps_ref[:, i, :] for i in range(4)], axis=1), as_t)
 
-    def chunk_out(ch):
-        for t in range(3):
-            drain(gr.at[3 * ch + t], pair_recv.at[3 * ch + t])
-        for t in range(3):
-            for yy in range(4):
-                for xx in range(4):
-                    s0[ch, xx, t, yy] = go[c, 3 * ch + t, yy, xx, 0] + gr[3 * ch + t, yy, xx, 0]
-                    s1[ch, yy, t, xx] = go[c, 3 * ch + t, yy, xx, 1] + gr[3 * ch + t, yy, xx, 1]
-        for d in (1, 3, 2):
-            xx, yy = xs[d], ys[d]
-            send(s0.at[ch, xx], r0.at[ch, d - 1], a_send.at[0], a_recv.at[ch], (y, zl, c, zh, xx))
-            send(s1.at[ch, yy], r1.at[ch, d - 1], a_send.at[1], a_recv.at[3 + ch], (yy, zl, c, zh, x))
-
-    def chunk_on(ch):
-        drain(r0.at[ch], a_recv.at[ch])
-        for t in range(3):
-            for yy in range(4):
-                t0[ch, yy, t] = (s0[ch, x, t, yy] + r0[ch, 0, t, yy]) + (r0[ch, 1, t, yy] + r0[ch, 2, t, yy])
-        for d in (1, 3, 2):
-            yy = ys[d]
-            send(t0.at[ch, yy], u0.at[ch, d - 1], b_send.at[0], b_recv.at[ch], (yy, zl, c, zh, x))
-        drain(r1.at[ch], a_recv.at[3 + ch])
-        for t in range(3):
-            for xx in range(4):
-                t1[ch, xx, t] = (s1[ch, y, t, xx] + r1[ch, 0, t, xx]) + (r1[ch, 1, t, xx] + r1[ch, 2, t, xx])
-        for d in (1, 3, 2):
-            xx = xs[d]
-            send(t1.at[ch, xx], u1.at[ch, d - 1], b_send.at[1], b_recv.at[3 + ch], (y, zl, c, zh, xx))
-
-    def chunk_in(ch):
-        drain(u0.at[ch], b_recv.at[ch])
-        drain(u1.at[ch], b_recv.at[3 + ch])
-        for t in range(3):
-            first = (t0[ch, y, t] + u0[ch, 0, t]) + (u0[ch, 1, t] + u0[ch, 2, t])
-            second = (t1[ch, x, t] + u1[ch, 0, t]) + (u1[ch, 1, t] + u1[ch, 2, t])
-            for w in range(8):
-                zs[w, 3 * ch + t : 3 * ch + t + 1, :] = first[w : w + 1, :]
-                zs[8 + w, 3 * ch + t : 3 * ch + t + 1, :] = second[w : w + 1, :]
-
-    for t in range(9):
-        a, b = t // 3 - 1, t % 3
-        grad = jnp.dot(xt[...], cb[b, 32 - 32 * a : 32 - 32 * a + CELLS, :], preferred_element_type=F32)
-        for yc in range(8):
-            for h in range(2):
-                parts = [grad[yc * 32 + i * 8 : yc * 32 + i * 8 + 8, h * 128 : h * 128 + 128] for i in range(4)]
-                for xx, part in enumerate(swap_groups(parts)):
-                    go[yc % 2, t, yc // 2, xx, h] = part
-        if t == 0:
-            pl.semaphore_wait(barrier, len(lines) + 2)
-            tell(0)
-        send(go.at[1 - c, t], gr.at[t], pair_send, pair_recv.at[t], (y, zl, 1 - c, zh, x))
-        if t == 4:
-            chunk_out(0)
-        if t == 7:
-            chunk_out(1)
-            learn(0)
-    chunk_out(2)
-    pending.append((go.at[0], pair_send))
-    pending.append((r0, a_send.at[0]))
-    pending.append((r1, a_send.at[1]))
     learn(1)
-    for ch in range(CHUNKS):
-        chunk_on(ch)
-    pending.append((u0, b_send.at[0]))
-    pending.append((u1, b_send.at[1]))
+    flow_on(0)
+    flow_on(1)
     learn(2)
     depth_send(as_t, ar_t, 0)
-    for ch in range(CHUNKS):
-        chunk_in(ch)
-
-    for d in STEPS:
-        send(zs.at[depths[d]], zr.at[d - 1], c_send, c_recv, at_depth(d))
+    flow_on(2)
+    flow_on(3)
+    flow_in(0)
+    flow_in(1)
+    depth_sum(1)
+    flow_in(2)
+    flow_in(3)
+    depth_sum(0)
+
     for half in range(2):
         depth_wait(ar_t, 0, half)
         plane_messages(ar_t, ks_t, half)
         plane_send(ks_t, kr_t, half, 4)
     drain(zr, c_recv)
     pending.append((zr, c_send))
-    block = zs[z]
+    block = zs[4]
     for d in range(DEPTH - 1):
         block = block + zr[d]
     gs[...] = block
@@ -354,7 +384,6 @@
         mat[0] = product(real_2, mix_first) - product(imag_2, mix_cross)
         mat[1] = product(real_2, mix_cross) + product(imag_2, mix_second)
 
-    back = lax.rem(20 - z, DEPTH)
     for yc in range(8):
         for m in range(2):
             low, high = [
@@ -443,14 +472,10 @@
             pltpu.VMEM((3, CELLS + 64, CHANNELS), BF16),
             vmem(2, 9, 4, 4, 2, 8, 128),
             vmem(9, 4, 4, 2, 8, 128),
-            vmem(3, 4, 3, 4, 8, 128),
-            vmem(3, 4, 3, 4, 8, 128),
-            vmem(3, 3, 3, 4, 8, 128),
-            vmem(3, 3, 3, 4, 8, 128),
-            vmem(3, 4, 3, 8, 128),
-            vmem(3, 4, 3, 8, 128),
-            vmem(3, 3, 3, 8, 128),
-            vmem(3, 3, 3, 8, 128),
+            *[vmem(4, len(places), 4, 8, 128) for _, _, places in FLOWS],
+            *[vmem(3, len(places), 4, 8, 128) for _, _, places in FLOWS],
+            *[vmem(4, len(places), 8, 128) for _, _, places in FLOWS],
+            *[vmem(3, len(places), 8, 128) for _, _, places in FLOWS],
             vmem(DEPTH, 9, 128),
             vmem(DEPTH - 1, 9, 128),
             vmem(9, 128),
@@ -471,10 +496,10 @@
             vmem(128, 128),
             pltpu.SemaphoreType.DMA,
             pltpu.SemaphoreType.DMA((9,)),
-            pltpu.SemaphoreType.DMA((2,)),
-            pltpu.SemaphoreType.DMA((6,)),
-            pltpu.SemaphoreType.DMA((2,)),
-            pltpu.SemaphoreType.DMA((6,)),
+            pltpu.SemaphoreType.DMA((4,)),
+            pltpu.SemaphoreType.DMA((4,)),
+            pltpu.SemaphoreType.DMA((4,)),
+            pltpu.SemaphoreType.DMA((4,)),
             pltpu.SemaphoreType.DMA,
             pltpu.SemaphoreType.DMA,
             pltpu.SemaphoreType.DMA((13,)),

time: 68.7 us -> 67.2 us (0.978)
  Pallas kernels: 67.1 us -> 65.6 us
    pallas_call x1, Pallas kernels: 67.1 us -> 65.6 us  [body(): pl.pallas_call(kernel, out_shape=jax.ShapeDtypeStruct((9, 128), F32), in_...]
where the time goes in v4:
time: 67.2 us; the launch traced here: 67 us
  Pallas kernels  65.6 us (98%)
  local copies, waits for them, and re-layouts  1.38 us (2%)
    pallas_call x1, Pallas kernels, body(): pl.pallas_call(kernel, out_shape=jax.ShapeDtypeStruct((9, 128), F32), in_...  65.6 us
    reshape x1, local copies, waits for them, and re-layouts, body(): return out.reshape(9, 4, 32)  1.38 us

profile of v4, /device:TPU:1, one launch (start us, length us, event | category | flops | bytes accessed | tf_op | source)
XLA Modules:
  0.0 67.0 jit_solution(9407210396385956906)
XLA Ops:
  0.0 65.6 %step.1 = f32[9,128]{1,0:T(8,128)} custom-call(bf16[1024,256]{1,0:T(8,128)(2,1)} %bitcast.2, bf16[1024,256]{1,0:T(8,128)(2,1)} %bitcast.3, f32[9,4,32]{2,1,0:T(4,128)} %taps_hbm.1), custom_call_target="tpu_custom_call" | custom-call | tf_op jit(solution)/shard_map/step/pallas_call | solution.py:462
  65.6 1.4 %reshape.11 = f32[9,4,32]{2,1,0:T(4,128)} reshape(f32[9,128]{1,0:T(8,128)} %step.1) | data formatting | bytes 9216 | tf_op jit(solution)/shard_map/reshape | solution.py:513
